TPU v7x, 64 devices: a 2x2x8 block of a 4x4x8 slice. The times are simulated.
64 devices in a mesh: prob: 4 (over x, y), feat: 16 (over z, core).
Axes of the slice: x: 2, y: 2, z: 8, core: 2. Of those that a mesh axis runs over, the one named last changes fastest.
The devices are a block of a 4x4x8 slice.
Arguments:
- x_mat: bfloat16 [32768, 16384], P('prob', 'feat'), parts along dimension 0
- w_init: float32 [65536, 2, 100], P(('prob', 'feat')), parts along dimension 0
- y_targ: float32 [32768, 2, 100], P('prob'), parts along dimension 0
- step_eta: float32 [65536], P(('prob', 'feat')), parts along dimension 0
Outputs:
- output 1: float32 [65536, 2, 100], P(('prob', 'feat')), parts along dimension 0
- output 2: float32 [32768, 2, 100], P('prob'), parts along dimension 0
There are 4 independent parts. A program takes and returns all parts, laid end to end along the dimension named above; each array names one.
All inputs are finite; a program needn't handle non-finite values.
Results may differ from a plain program's by a relative error of at most 0.00406533.
Values are sent between devices in bfloat16 or wider.
A program may use at most 768 MiB of HBM per device.

v0:
```python
import jax
import jax.numpy as jnp
from jax import lax
from jax.sharding import PartitionSpec as P, NamedSharding

SWEEPS = 4


def solution(mesh):
    def per_device(x_blk, w_blk, y_blk, eta_blk):
        row_count, block_width = x_blk.shape
        targets = y_blk.shape[2]
        flat_width = 2 * targets
        ridge_wt = jnp.array([0.1, 1.0], jnp.float32).reshape(1, 2, 1)
        eta_col = eta_blk.reshape(block_width, 1, 1)

        def reduced_product(w_part):
            w_half = w_part.astype(jnp.bfloat16).reshape(block_width, flat_width)
            block_prod = jnp.dot(x_blk, w_half, preferred_element_type=jnp.float32).astype(jnp.bfloat16)
            summed = lax.psum(block_prod.astype(jnp.float32), "feat")
            return summed.reshape(row_count, 2, targets)

        w_cur = w_blk
        residual = y_blk - reduced_product(w_blk)
        for sweep_idx in range(SWEEPS):
            r_half = residual.astype(jnp.bfloat16).reshape(row_count, flat_width)
            gradient = lax.dot_general(x_blk, r_half, (((0,), (0,)), ((), ())), preferred_element_type=jnp.float32)
            gradient = gradient.reshape(block_width, 2, targets) / row_count
            w_step = eta_col * (gradient - ridge_wt * w_cur)
            w_cur = w_cur + w_step
            residual = residual - reduced_product(w_step)
        return w_cur, residual

    x_spec = P("prob", "feat")
    w_spec = P(("prob", "feat"), None, None)
    y_spec = P("prob", None, None)
    e_spec = P(("prob", "feat"))
    return jax.shard_map(per_device, mesh=mesh, in_specs=(x_spec, w_spec, y_spec, e_spec), out_specs=(w_spec, y_spec), check_vma=False)
```

profile of v0, /device:TPU:21, one launch (start us, length us, event | category | flops | bytes accessed | tf_op | source)
XLA Modules:
  0.0 853.1 jit_solution(5993028578713659163)
XLA Ops:
  8.9 14.0 %fusion = f32[8192,200]{0,1:T(8,128)} fusion(bf16[8192,1024]{1,0:T(8,128)(2,1)} %param.5, bf16[1024,200]{0,1:T(8,128)(2,1)S(1)} %reshape.62), kind=kOutput, calls=%fused_computation.5 | convolution fusion | flops 3358720000 | bytes 23740416 | tf_op jit(solution)/shard_map/dot_general | solution.py:19
  22.9 6.3 reshape.63
  29.6 126.7 %all-reduce.6.cloned.1.call-done = f32[8192,2,100]{0,2,1:T(8,128)} async-done(((f32[8192,2,100]{0,2,1:T(8,128)}), f32[8192,2,100]{0,2,1:T(8,128)}) %all-reduce.6.cloned.1.call-update) | async-done | bytes 6553616 | tf_op jit(solution)/shard_map/psum | solution.py:20
  156.3 8.5 %fusion.10 = bf16[8192,2,100]{0,2,1:T(8,128)(2,1)S(1)} fusion(f32[8192,2,100]{0,2,1:T(8,128)} %all-reduce.6.cloned.1.call-done, f32[8192,2,100]{0,1,2:T(2,128)} %param.7), kind=kLoop, calls=%fused_computation.16 | loop fusion | flops 3276800 | bytes 16384000 | tf_op jit(solution)/shard_map/convert_element_type | solution.py:26
  167.3 8.7 %fusion.14 = f32[1024,200]{0,1:T(8,128)S(1)} fusion(bf16[8192,200]{0,1:T(8,128)(2,1)} %reshape.64, bf16[8192,1024]{1,0:T(8,128)(2,1)} %param.5), kind=kOutput, calls=%fused_computation.24 | convolution fusion | flops 3355648000 | bytes 20873216 | tf_op jit(solution)/shard_map/dot_general | solution.py:27
  176.5 14.0 %fusion.2 = f32[8192,200]{0,1:T(8,128)} fusion(bf16[1024,200]{0,1:T(8,128)(2,1)S(1)} %reshape.65, bf16[8192,1024]{1,0:T(8,128)(2,1)} %param.5), kind=kOutput, calls=%fused_computation.7 | convolution fusion | flops 3358720000 | bytes 23740416 | tf_op jit(solution)/shard_map/dot_general | solution.py:19
  190.5 6.3 reshape.66
  197.4 122.7 %all-reduce.8.cloned.1.call-done = f32[8192,2,100]{0,2,1:T(8,128)} async-done(((f32[8192,2,100]{0,2,1:T(8,128)}), f32[8192,2,100]{0,2,1:T(8,128)}) %all-reduce.8.cloned.1.call-update) | async-done | bytes 6553616 | tf_op jit(solution)/shard_map/psum | solution.py:20
  320.0 10.8 %fusion.23 = bf16[8192,2,100]{0,2,1:T(8,128)(2,1)S(1)} fusion(f32[8192,2,100]{0,2,1:T(8,128)} %all-reduce.8.cloned.1.call-done, f32[8192,2,100]{0,2,1:T(8,128)} %all-reduce.6.cloned.1.call-done, f32[8192,2,100]{0,1,2:T(2,128)} %param.7), kind=kLoop, calls=%fused_computation.38 | loop fusion | flops 4915200 | bytes 22937600 | tf_op jit(solution)/shard_map/convert_element_type | solution.py:26
  333.3 8.7 %fusion.13 = f32[1024,200]{0,1:T(8,128)S(1)} fusion(bf16[8192,200]{0,1:T(8,128)(2,1)} %reshape.67, bf16[8192,1024]{1,0:T(8,128)(2,1)} %param.5), kind=kOutput, calls=%fused_computation.22 | convolution fusion | flops 3355648000 | bytes 20873216 | tf_op jit(solution)/shard_map/dot_general | solution.py:27
  342.6 13.9 %fusion.4 = f32[8192,200]{0,1:T(8,128)} fusion(bf16[1024,200]{0,1:T(8,128)(2,1)S(1)} %reshape.68, bf16[8192,1024]{1,0:T(8,128)(2,1)} %param.5), kind=kOutput, calls=%fused_computation.9 | convolution fusion | flops 3358720000 | bytes 23740416 | tf_op jit(solution)/shard_map/dot_general | solution.py:19
  356.5 6.3 reshape.69
  363.0 123.0 %all-reduce.10.cloned.1.call-done = f32[8192,2,100]{0,2,1:T(8,128)} async-done(((f32[8192,2,100]{0,2,1:T(8,128)}), f32[8192,2,100]{0,2,1:T(8,128)}) %all-reduce.10.cloned.1.call-update) | async-done | bytes 6553616 | tf_op jit(solution)/shard_map/psum | solution.py:20
  486.1 13.6 %fusion.26 = (bf16[8192,2,100]{0,2,1:T(8,128)(2,1)S(1)}, f32[8192,2,100]{0,2,1:T(8,128)}) fusion(f32[8192,2,100]{0,2,1:T(8,128)} %all-reduce.10.cloned.1.call-done, f32[8192,2,100]{0,2,1:T(8,128)} %all-reduce.8.cloned.1.call-done, f32[8192,2,100]{0,2,1:T(8,128)} %all-reduce.6.cloned.1.call-done, f32[8192,2,100]{0,1,2:T(2,128)} %param.7), kind=kLoop, calls=%fused_computation.40 | loop fusion | flops 6553600 | bytes 36044800 | tf_op jit(solution)/shard_map/convert_element_type | solution.py:26
  502.1 11.3 %fusion.12 = f32[1024,200]{0,1:T(8,128)} fusion(bf16[8192,200]{0,1:T(8,128)(2,1)} %reshape.70, bf16[8192,1024]{1,0:T(8,128)(2,1)} %param.5), kind=kOutput, calls=%fused_computation.20 | convolution fusion | flops 3355648000 | bytes 20873216 | tf_op jit(solution)/shard_map/dot_general | solution.py:27
  517.4 13.9 %fusion.6 = f32[8192,200]{0,1:T(8,128)} fusion(bf16[1024,200]{0,1:T(8,128)(2,1)S(1)} %reshape.71, bf16[8192,1024]{1,0:T(8,128)(2,1)} %param.5), kind=kOutput, calls=%fused_computation.11 | convolution fusion | flops 3358720000 | bytes 23740416 | tf_op jit(solution)/shard_map/dot_general | solution.py:19
  531.3 6.4 reshape.72
  537.8 123.2 %all-reduce.12.cloned.1.call-done = f32[8192,2,100]{0,2,1:T(8,128)} async-done(((f32[8192,2,100]{0,2,1:T(8,128)}), f32[8192,2,100]{0,2,1:T(8,128)}) %all-reduce.12.cloned.1.call-update) | async-done | bytes 6553616 | tf_op jit(solution)/shard_map/psum | solution.py:20
  661.0 9.0 %fusion.24 = (bf16[8192,2,100]{0,2,1:T(8,128)(2,1)S(1)}, f32[8192,2,100]{0,2,1:T(8,128)}) fusion(f32[8192,2,100]{0,2,1:T(8,128)} %get-tuple-element.9, f32[8192,2,100]{0,2,1:T(8,128)} %all-reduce.12.cloned.1.call-done), kind=kLoop, calls=%fused_computation.39 | loop fusion | flops 3276800 | bytes 22937600 | tf_op jit(solution)/shard_map/convert_element_type | solution.py:26
  672.4 8.9 %fusion.11 = f32[1024,200]{0,1:T(8,128)S(1)} fusion(bf16[8192,200]{0,1:T(8,128)(2,1)} %reshape.73, bf16[8192,1024]{1,0:T(8,128)(2,1)} %param.5), kind=kOutput, calls=%fused_computation.18 | convolution fusion | flops 3355648000 | bytes 20873216 | tf_op jit(solution)/shard_map/dot_general | solution.py:27
  683.7 13.9 %fusion.8 = f32[8192,200]{0,1:T(8,128)} fusion(bf16[1024,200]{0,1:T(8,128)(2,1)S(1)} %reshape.74, bf16[8192,1024]{1,0:T(8,128)(2,1)} %param.5), kind=kOutput, calls=%fused_computation.13 | convolution fusion | flops 3358720000 | bytes 23740416 | tf_op jit(solution)/shard_map/dot_general | solution.py:19
  705.4 121.6 %all-reduce.14.cloned.1.call-done = f32[8192,2,100]{0,2,1:T(8,128)} async-done(((f32[8192,2,100]{0,2,1:T(8,128)}), f32[8192,2,100]{0,2,1:T(8,128)}) %all-reduce.14.cloned.1.call-update) | async-done | bytes 6553616 | tf_op jit(solution)/shard_map/psum | solution.py:20
  827.0 8.5 %sub.35 = f32[8192,2,100]{0,2,1:T(8,128)} subtract(f32[8192,2,100]{0,2,1:T(8,128)} %get-tuple-element.5, f32[8192,2,100]{0,2,1:T(8,128)} %all-reduce.14.cloned.1.call-done) | non-fusion elementwise | flops 1638400 | bytes 19660800 | tf_op jit(solution)/shard_map/sub | solution.py:31
  835.5 10.8 %copy.21 = f32[8192,2,100]{0,1,2:T(2,128)} copy(f32[8192,2,100]{0,2,1:T(8,128)} %sub.35) | data formatting | bytes 13107200
  (57 shorter events, 27.7 us)
Async XLA Ops:
  7.2 149.1 %all-reduce.6.cloned.1.call-start = ((), (), s32[]{:S(2)}) async-start(), calls=%async_computation | async-start | bytes 13631488 | tf_op jit(solution)/shard_map/psum | solution.py:20
  29.3 290.7 %all-reduce.8.cloned.1.call-start = ((), (), s32[]{:S(2)}) async-start(), calls=%async_computation.1 | async-start | bytes 13631488 | tf_op jit(solution)/shard_map/psum | solution.py:20
  167.3 8.8 %copy-start.3 = (f32[1024,2,100]{0,1,2:T(2,128)S(1)}, f32[1024,2,100]{0,1,2:T(2,128)}, u32[]{:S(2)}) copy-start(f32[1024,2,100]{0,1,2:T(2,128)} %param.6) | copy-start | bytes 2457604
  167.3 8.8 %copy-start.11 = (f32[1024]{0:T(1024)S(1)}, f32[1024]{0:T(1024)}, u32[]{:S(2)}) copy-start(f32[1024]{0:T(1024)} %param.8) | copy-start | bytes 12292
  167.3 8.8 %copy-start.12 = (f32[2]{0:T(128)S(1)}, f32[2]{0:T(128)}, u32[]{:S(2)}) copy-start(f32[2]{0:T(128)} %constant.8.clone) | copy-start | bytes 28
  176.0 14.4 %copy-start = (f32[1024,2,100]{0,2,1:T(8,128)}, f32[1024,2,100]{0,2,1:T(8,128)S(1)}, u32[]{:S(2)}) copy-start(f32[1024,2,100]{0,2,1:T(8,128)S(1)} %div.30) | copy-start | bytes 2457604
  196.9 289.2 %all-reduce.10.cloned.1.call-start = ((), (), s32[]{:S(2)}) async-start(), calls=%async_computation.2 | async-start | bytes 13631488 | tf_op jit(solution)/shard_map/psum | solution.py:20
  333.3 8.8 %copy-start.1 = (f32[1024,2,100]{0,2,1:T(8,128)S(1)}, f32[1024,2,100]{0,2,1:T(8,128)}, u32[]{:S(2)}) copy-start(f32[1024,2,100]{0,2,1:T(8,128)} %copy-done) | copy-start | bytes 2457604
  333.3 8.8 %copy-start.4 = (f32[1024,2,100]{0,1,2:T(2,128)S(1)}, f32[1024,2,100]{0,1,2:T(2,128)}, u32[]{:S(2)}) copy-start(f32[1024,2,100]{0,1,2:T(2,128)} %param.6) | copy-start | bytes 2457604
  342.1 14.4 %copy-start.8 = (f32[1024,2,100]{0,2,1:T(8,128)}, f32[1024,2,100]{0,2,1:T(8,128)S(1)}, u32[]{:S(2)}) copy-start(f32[1024,2,100]{0,2,1:T(8,128)S(1)} %div.33) | copy-start | bytes 2457604
  363.0 298.0 %all-reduce.12.cloned.1.call-start = ((), (), s32[]{:S(2)}) async-start(), calls=%async_computation.3 | async-start | bytes 13631488 | tf_op jit(solution)/shard_map/psum | solution.py:20
  502.1 12.6 %copy-start.2 = (f32[1024,2,100]{0,2,1:T(8,128)S(1)}, f32[1024,2,100]{0,2,1:T(8,128)}, u32[]{:S(2)}) copy-start(f32[1024,2,100]{0,2,1:T(8,128)} %copy-done) | copy-start | bytes 2457604
  502.1 12.6 %copy-start.5 = (f32[1024,2,100]{0,1,2:T(2,128)S(1)}, f32[1024,2,100]{0,1,2:T(2,128)}, u32[]{:S(2)}) copy-start(f32[1024,2,100]{0,1,2:T(2,128)} %param.6) | copy-start | bytes 2457604
  502.1 12.6 %copy-start.9 = (f32[1024,2,100]{0,2,1:T(8,128)S(1)}, f32[1024,2,100]{0,2,1:T(8,128)}, u32[]{:S(2)}) copy-start(f32[1024,2,100]{0,2,1:T(8,128)} %copy-done.8) | copy-start | bytes 2457604
  514.7 16.6 %copy-start.6 = (f32[1024,2,100]{0,2,1:T(8,128)}, f32[1024,2,100]{0,2,1:T(8,128)S(1)}, u32[]{:S(2)}) copy-start(f32[1024,2,100]{0,2,1:T(8,128)S(1)} %div.36) | copy-start | bytes 2457604
  537.7 289.3 %all-reduce.14.cloned.1.call-start = ((), (), s32[]{:S(2)}) async-start(), calls=%async_computation.4 | async-start | bytes 13631488 | tf_op jit(solution)/shard_map/psum | solution.py:20
  672.4 9.0 %copy-start.7 = (f32[1024,2,100]{0,2,1:T(8,128)S(1)}, f32[1024,2,100]{0,2,1:T(8,128)}, u32[]{:S(2)}) copy-start(f32[1024,2,100]{0,2,1:T(8,128)} %copy-done.6) | copy-start | bytes 2457604
  672.4 9.0 %copy-start.10 = (f32[1024,2,100]{0,2,1:T(8,128)S(1)}, f32[1024,2,100]{0,2,1:T(8,128)}, u32[]{:S(2)}) copy-start(f32[1024,2,100]{0,2,1:T(8,128)} %get-tuple-element.7) | copy-start | bytes 2457604
Sparse Core Ops, SparseCore 0:
  29.4 126.7 all-reduce.5
  197.0 122.9 all-reduce.7
  363.1 122.9 all-reduce.9
  537.9 123.0 all-reduce.11
  704.0 122.9 all-reduce.13
where the time goes:
time: 858 us; the launch traced here: 853 us
  waiting for transfers between devices  617 us (72%)
  matrix products  107 us (12%)
  local copies, waits for them, and re-layouts  57.8 us (7%)
  other arithmetic  55.3 us (6%)
  between operations  14.3 us (2%)
    psum x5, waiting for transfers between devices, reduced_product(): summed = lax.psum(block_prod.astype(jnp.float32), 'feat')  617 us
    dot_general x5, matrix products, reduced_product(): jnp.dot(x_blk, w_half, preferred_element_type=jnp.float32)  69.7 us
    convert_element_type x4, other arithmetic, per_device(): r_half = residual.astype(jnp.bfloat16).reshape(row_count, flat_width)  41.9 us
    dot_general x4, matrix products, per_device(): lax.dot_general(x_blk, r_half, (((0,), (0,)), ((), ())), preferred_elemen...  37.6 us
    reshape x5, local copies, waits for them, and re-layouts, reduced_product(): return summed.reshape(row_count, 2, targets)  31.6 us
  transfers between devices with their start and end apart: 5, of which 5 were waited for; matrix products, arithmetic and copies ran while one was open for 0% of the time, Pallas kernels for 0%

commit v1 on v0

v1 whole, which is shorter than its diff:
```python
import functools

import jax
import jax.numpy as jnp
from jax import lax
from jax.experimental import pallas as pl
from jax.experimental.pallas import tpu as pltpu
from jax.sharding import PartitionSpec as P

SWEEPS = 4
MESH = pl.DeviceIdType.MESH


def _kernel(cfg, x_in, w_in, eta_in, y_in, w_res, r_res,
            xo, xp, pf, rup, rdn, gat, w, g, dwb, eta, res, rf,
            xo_sem, xs_sem, xr_sem, in_sem,
            rsu_s, rsu_r, rsd_s, rsd_r,
            agu_s, agu_r, agd_s, agd_r,
            fgu_s, fgu_r, fgd_s, fgd_r,
            po_s, po_r, lo_s, wo_sem):
    Z, KP, KB, H, DP, N, lams = cfg
    hops = Z - 1
    half_ring = Z // 2
    me = lax.axis_index("feat")
    z = lax.div(me, 2)
    c = lax.rem(me, 2)
    up = {"feat": lax.rem(z + 1, Z) * 2 + c}
    dn = {"feat": lax.rem(z + Z - 1, Z) * 2 + c}
    pal = {"feat": me + 1 - 2 * c}

    def chunk(off, half):
        return lax.rem(z + off + Z, Z) * 2 + half

    def up_chunk(m):
        return chunk(half_ring - lax.div(m + 1, 2), lax.rem(m, 2))

    def dn_chunk(m):
        return chunk(lax.div(m + 1, 2) - half_ring, 1 - lax.rem(m, 2))

    def remote(src, dst, ss, rs, dev):
        return pltpu.make_async_remote_copy(src_ref=src, dst_ref=dst, send_sem=ss, recv_sem=rs,
                                            device_id=dev, device_id_type=MESH)

    local = pltpu.make_async_copy

    in_copies = [local(w_in.at[c], w.at[0], in_sem.at[0]),
                 local(eta_in, eta.at[0], in_sem.at[1]),
                 local(y_in, res, in_sem.at[2])]
    for cp in in_copies:
        cp.start()

    def xo_copy(k):
        return local(x_in.at[k], xo.at[k], xo_sem.at[k])

    def xp_copy(k):
        return remote(x_in.at[k], xp.at[k], xs_sem.at[k], xr_sem.at[k], pal)

    def start_xo(m, _):
        xo_copy(up_chunk(m)).start()
        xo_copy(dn_chunk(m)).start()
        return 0
    lax.fori_loop(0, Z, start_xo, 0)

    bar = pltpu.get_barrier_semaphore()
    for dev in (up, dn, pal):
        pl.semaphore_signal(bar, inc=1, device_id=dev, device_id_type=MESH)
    pl.semaphore_wait(bar, 3)

    w_x = remote(w_in.at[1 - c], w.at[1], in_sem.at[3], in_sem.at[4], pal)
    e_x = remote(eta_in, eta.at[1], in_sem.at[5], in_sem.at[6], pal)
    w_x.start()
    e_x.start()

    def start_xp(m, _):
        xp_copy(up_chunk(m)).start()
        xp_copy(dn_chunk(m)).start()
        return 0
    lax.fori_loop(0, Z, start_xp, 0)

    for cp in in_copies:
        cp.wait()
    w_x.wait()
    e_x.wait()

    def to_half(v):
        return jnp.concatenate([v, jnp.zeros((KB - KP, v.shape[1]), jnp.float32)], axis=0).astype(jnp.bfloat16)

    for b in range(2):
        dwb[b] = to_half(w[b])

    CB = 256

    def product(k):
        for j in range(H // CB if H >= CB else 1):
            cols = pl.ds(j * CB, min(CB, H))
            total = None
            for b, xx in ((0, xo), (1, xp)):
                part = lax.dot_general(dwb[b], xx[k, cols, :], (((1,), (1,)), ((), ())),
                                       preferred_element_type=jnp.float32)
                part = part.astype(jnp.bfloat16).astype(jnp.float32)
                total = part if total is None else total + part
            pf[k, :, cols] = total[:KP]

    def gradient(k):
        rows = gat[k]
        for b, xx in ((0, xo), (1, xp)):
            for j in range(DP // CB):
                cols = pl.ds(j * CB, CB)
                part = jnp.dot(rows, xx[k, :, cols], preferred_element_type=jnp.float32)
                g[b, :, cols] += part[:KP]

    def rs_up(m, src):
        return remote(src, rup.at[m], rsu_s.at[m], rsu_r.at[m], up)

    def rs_dn(m, src):
        return remote(src, rdn.at[m], rsd_s.at[m], rsd_r.at[m], dn)

    def ring_step(m, t, with_recv, with_send):
        ku, kd = up_chunk(m), dn_chunk(m)

        @pl.when(t == 0)
        def _():
            for k in (ku, kd):
                xo_copy(k).wait()
                xp_copy(k).wait_recv()
        product(ku)
        if with_send and not with_recv:
            rs_up(m, pf.at[ku]).start()
        product(kd)
        if with_send and not with_recv:
            rs_dn(m, pf.at[kd]).start()
        if with_recv:
            s = m - 2
            rs_up(s, rup.at[s]).wait_recv()
            rup[s] += pf[ku]
            rs_up(m, rup.at[s]).start()
            rs_dn(s, rdn.at[s]).wait_recv()
            rdn[s] += pf[kd]
            rs_dn(m, rdn.at[s]).start()

    def reduce_round(t):
        def first(m, _):
            ring_step(m, t, False, True)
            return 0

        def rest(m, _):
            ring_step(m, t, True, True)
            return 0
        lax.fori_loop(0, 2, first, 0)
        lax.fori_loop(2, hops, rest, 0)
        ring_step(hops, t, False, False)
        g[...] = jnp.zeros_like(g)
        a, b = hops - 2, hops - 1
        rs_up(a, rup.at[a]).wait_recv()
        rs_dn(a, rdn.at[a]).wait_recv()
        rs_up(b, rup.at[b]).wait_recv()
        k0, k1 = chunk(0, 0), chunk(0, 1)
        res[0] = res[0] - (rup[b] + rdn[a] + pf[k0])
        rs_dn(b, rdn.at[b]).wait_recv()
        res[1] = res[1] - (rup[a] + rdn[b] + pf[k1])

        def drain(m, _):
            rs_up(m, rup.at[m]).wait_send()
            rs_dn(m, rdn.at[m]).wait_send()
            return 0
        lax.fori_loop(0, hops, drain, 0)

    def gather_ring(buf, us, ur, ds, dr, seen):
        def send_up(m, k):
            return remote(buf.at[k], buf.at[k], us.at[m], ur.at[m], up)

        def send_dn(m, k):
            return remote(buf.at[k], buf.at[k], ds.at[m], dr.at[m], dn)
        k0, k1 = chunk(0, 0), chunk(0, 1)
        send_up(0, k0).start()
        send_dn(0, k1).start()
        send_up(1, k1).start()
        send_dn(1, k0).start()
        seen(k0)
        seen(k1)

        def step(m, _):
            far = lax.div(m, 2) + 1
            ku, kd = chunk(-far, lax.rem(m, 2)), chunk(far, 1 - lax.rem(m, 2))
            send_up(m, ku).wait_recv()

            @pl.when(m < hops - 2)
            def _():
                send_up(m + 2, ku).start()
            send_dn(m, kd).wait_recv()

            @pl.when(m < hops - 2)
            def _():
                send_dn(m + 2, kd).start()
            seen(ku)
            seen(kd)
            return 0
        lax.fori_loop(0, hops, step, 0)

        def drain(m, _):
            send_up(m, k0).wait_send()
            send_dn(m, k0).wait_send()
            return 0
        lax.fori_loop(0, hops, drain, 0)

    lam = jnp.where(c == 0, jnp.float32(lams[0]), jnp.float32(lams[1]))

    def one_round(t, _):
        reduce_round(t)

        @pl.when(t < SWEEPS)
        def _():
            for h in range(2):
                gat[chunk(0, h)] = to_half(res[h])
            gather_ring(gat, agu_s, agu_r, agd_s, agd_r, gradient)
            for b in range(2):
                for j in range(DP // CB):
                    cols = pl.ds(j * CB, CB)
                    old = w[b, :, cols]
                    step = eta[b, 0:1, cols] * (g[b, :, cols] * (1.0 / N) - lam * old)
                    w[b, :, cols] = old + step
                    dwb[b, :, cols] = to_half(step)
        return 0

    lax.fori_loop(0, SWEEPS + 1, one_round, 0)

    w_own = local(w.at[0], w_res.at[c], wo_sem.at[0])
    w_pal = remote(w.at[1], w_res.at[c], wo_sem.at[1], wo_sem.at[2], pal)
    w_own.start()
    w_pal.start()
    for h in range(2):
        rf[chunk(0, h)] = res[h]

    def out_local(k):
        return local(rf.at[k], r_res.at[c, k], lo_s.at[k])

    def out_pal(k):
        return remote(rf.at[k], r_res.at[c, k], po_s.at[k], po_r.at[k], pal)

    def emit(k):
        out_pal(k).start()
        out_local(k).start()
    gather_ring(rf, fgu_s, fgu_r, fgd_s, fgd_r, emit)

    def finish(k, _):
        out_local(k).wait()
        out_pal(k).wait()
        xp_copy(k).wait_send()
        return 0
    lax.fori_loop(0, 2 * Z, finish, 0)
    w_own.wait()
    w_pal.wait()


def _fused(x, wt, eta, ysh, Z, KP, KB, H, DP, N):
    hops = Z - 1
    any_spec = pl.BlockSpec(memory_space=pl.ANY)
    f32, b16 = jnp.float32, jnp.bfloat16
    dma = pltpu.SemaphoreType.DMA
    cfg = (Z, KP, KB, H, DP, N, (0.1, 1.0))
    scratch = [
        pltpu.VMEM((2 * Z, H, DP), b16), pltpu.VMEM((2 * Z, H, DP), b16),
        pltpu.VMEM((2 * Z, KP, H), f32),
        pltpu.VMEM((hops, KP, H), f32), pltpu.VMEM((hops, KP, H), f32),
        pltpu.VMEM((2 * Z, KB, H), b16),
        pltpu.VMEM((2, KP, DP), f32), pltpu.VMEM((2, KP, DP), f32), pltpu.VMEM((2, KB, DP), b16),
        pltpu.VMEM((2, 8, DP), f32), pltpu.VMEM((2, KP, H), f32),
        pltpu.VMEM((2 * Z, KP, H), f32),
        dma((2 * Z,)), dma((2 * Z,)), dma((2 * Z,)), dma((7,)),
    ] + [dma((hops,))] * 12 + [dma((2 * Z,)), dma((2 * Z,)), dma((2 * Z,)), dma((3,))]
    flops = (SWEEPS * 2 + 1) * 2 * N * DP * 2 * KP
    return pl.pallas_call(
        functools.partial(_kernel, cfg),
        out_shape=(jax.ShapeDtypeStruct((2, KP, DP), f32), jax.ShapeDtypeStruct((2, 2 * Z, KP, H), f32)),
        in_specs=[any_spec] * 4,
        out_specs=(any_spec, any_spec),
        scratch_shapes=scratch,
        compiler_params=pltpu.CompilerParams(collective_id=0, has_side_effects=True, vmem_limit_bytes=64000000),
        cost_estimate=pl.CostEstimate(flops=flops, bytes_accessed=2 * N * DP * 2, transcendentals=0),
    )(x, wt, eta, ysh)


def solution(mesh):
    Z = mesh.shape["feat"] // 2

    def per_device(x_blk, w_blk, y_blk, eta_blk):
        N, DP = x_blk.shape
        K = y_blk.shape[2]
        KP = -(-K // 8) * 8
        KB = -(-K // 16) * 16
        H = N // (2 * Z)
        me = lax.axis_index("feat")
        z, c = me // 2, me % 2
        wt = jnp.pad(jnp.transpose(w_blk, (1, 2, 0)), ((0, 0), (0, KP - K), (0, 0)))
        ysh = lax.dynamic_slice(y_blk, (z * 2 * H, c, 0), (2 * H, 1, K)).reshape(2, H, K)
        ysh = jnp.pad(jnp.transpose(ysh, (0, 2, 1)), ((0, 0), (0, KP - K), (0, 0)))
        eta = jnp.broadcast_to(eta_blk[None, :], (8, DP))
        w_t, r_t = _fused(x_blk.reshape(2 * Z, H, DP), wt, eta, ysh, Z, KP, KB, H, DP, N)
        w_new = jnp.transpose(w_t[:, :K, :], (2, 0, 1))
        r_new = jnp.transpose(r_t[:, :, :K, :], (1, 3, 0, 2)).reshape(N, 2, K)
        return w_new, r_new

    x_spec = P("prob", "feat")
    w_spec = P(("prob", "feat"), None, None)
    y_spec = P("prob", None, None)
    e_spec = P(("prob", "feat"))
    return jax.shard_map(per_device, mesh=mesh, in_specs=(x_spec, w_spec, y_spec, e_spec),
                         out_specs=(w_spec, y_spec), check_vma=False)
```

time: 858 us -> 330 us (0.38)
  waiting for transfers between devices: 617 us -> 0 us
  Pallas kernels: 0 us -> 299 us
  matrix products: 107 us -> 0 us
  other arithmetic: 55.3 us -> 0 us
  local copies, waits for them, and re-layouts: 57.8 us -> 29.6 us
  between operations: 14.3 us -> 0.71 us
    psum x5 -> x0, waiting for transfers between devices: 617 us -> none  [reduced_product(): summed = lax.psum(block_prod.astype(jnp.float32), 'feat')]
    pallas_call x0 -> x1, Pallas kernels: none -> 299 us  [_fused(): pl.pallas_call(functools.partial(_kernel, cfg), out_shape=(jax.ShapeDtype...]
    dot_general x9 -> x0, matrix products: 107 us -> none  [the longest x5 69.7 us: reduced_product(): jnp.dot(x_blk, w_half, preferred_element_type=jnp.float32)]
    convert_element_type x9 -> x0, other arithmetic: 46.8 us -> none  [the longest x4 41.9 us: per_device(): r_half = residual.astype(jnp.bfloat16).reshape(row_count, flat_width)]
    reshape x14 -> x2, local copies, waits for them, and re-layouts: 43.9 us -> 0.42 us  [per_device(): lax.dynamic_slice(y_blk, (z * 2 * H, c, 0), (2 * H, 1, K)).reshape(2, H, K)]
    unnamed x28 -> x4, local copies, waits for them, and re-layouts: 12.3 us -> 18.8 us
  transfers between devices with their start and end apart: 5 -> 0, of which waited for: 5 -> 0; matrix products, arithmetic and copies ran while one was open for 0% -> 0% of each run, Pallas kernels for 0% -> 0%
where the time goes in v1:
time: 330 us; the launch traced here: 329 us
  Pallas kernels  299 us (91%)
  local copies, waits for them, and re-layouts  29.6 us (9%)
    pallas_call x1, Pallas kernels, _fused(): pl.pallas_call(functools.partial(_kernel, cfg), out_shape=(jax.ShapeDtype...  299 us
    unnamed x4, local copies, waits for them, and re-layouts  18.8 us

profile of v1, /device:TPU:21, one launch (start us, length us, event | category | flops | bytes accessed | tf_op | source)
XLA Modules:
  0.0 329.5 jit_solution(11509250727626254038)
XLA Ops:
  0.7 1.3 broadcast_in_dim.2.eta_in
  1.9 2.4 dynamic-slice_reduce_fusion
  4.3 0.3 reshape.15
  4.7 0.1 copy.18
  4.8 0.8 pad.9.y_in
  5.6 1.4 copy.17
  7.0 1.0 pad.8.w_in
  8.0 299.2 %shard_map.59 = (f32[2,104,1024]{2,1,0:T(8,128)}, f32[2,16,104,512]{3,2,1,0:T(8,128)}) custom-call(bf16[16,512,1024]{2,1,0:T(8,128)(2,1)} %bitcast.19, f32[2,104,1024]{2,1,0:T(8,128)} %pad.8.w_in, f32[8,1024]{1,0:T(8,128)} %broadcast_in_dim.2.eta_in, f32[2,104,512]{2,1,0:T(8,128)} %pad.9.y_in), custom_call_target="tpu_custom_call" | custom-call | flops 31406948352 | bytes 33554432 | tf_op jit(solution)/shard_map/pallas_call | solution.py:272
  307.1 1.2 slice_bitcast_fusion.1
  308.4 1.5 copy.11
  309.9 3.7 %slice_bitcast_fusion = f32[16,512,2,100]{1,3,0,2:T(8,128)S(1)} fusion(f32[2,16,104,512]{3,2,1,0:T(8,128)} %get-tuple-element.5), kind=kLoop, calls=%fused_computation | loop fusion | bytes 13107200 | tf_op jit(solution)/shard_map/transpose | solution.py:300
  313.6 6.5 %copy.13 = f32[16,512,2,100]{1,0,2,3:T(8,128)} copy(f32[16,512,2,100]{1,3,0,2:T(8,128)S(1)} %slice_bitcast_fusion) | data formatting | bytes 13107200
  320.1 9.3 %reshape.17 = f32[8192,2,100]{0,1,2:T(2,128)} reshape(f32[16,512,2,100]{1,0,2,3:T(8,128)} %copy.13) | data formatting | bytes 13107200

commit v2 on v1

--- a/solution.py
+++ b/solution.py
@@ -8,6 +8,8 @@
 from jax.sharding import PartitionSpec as P
 
 SWEEPS = 4
+LAMS = (0.1, 1.0)
+STAGGER = 2
 MESH = pl.DeviceIdType.MESH
 
 
@@ -17,8 +19,9 @@
             rsu_s, rsu_r, rsd_s, rsd_r,
             agu_s, agu_r, agd_s, agd_r,
             fgu_s, fgu_r, fgd_s, fgd_r,
-            po_s, po_r, lo_s, wo_sem):
-    Z, KP, KB, H, DP, N, lams = cfg
+            po_s, po_r, lo_s, wo_sem, raw, yraw, flat, go_sem):
+    Z, KS, KP, KB, H, DP, N = cfg
+    K = w_in.shape[0]
     hops = Z - 1
     half_ring = Z // 2
     me = lax.axis_index("feat")
@@ -41,11 +44,41 @@
         return pltpu.make_async_remote_copy(src_ref=src, dst_ref=dst, send_sem=ss, recv_sem=rs,
                                             device_id=dev, device_id_type=MESH)
 
+    class Split:
+        def __init__(self, make):
+            self.make = make
+
+        def do(self, act):
+            @pl.when(c == 0)
+            def _():
+                act(self.make(0))
+
+            @pl.when(c == 1)
+            def _():
+                act(self.make(1))
+
+        def start(self):
+            self.do(lambda cp: cp.start())
+
+        def wait(self):
+            self.do(lambda cp: cp.wait())
+
+        def wait_send(self):
+            self.do(lambda cp: cp.wait_send())
+
+        def wait_recv(self):
+            self.do(lambda cp: cp.wait_recv())
+
+    rows32 = (pl.ds(0, KS), pl.ds(0, KP))
+    rows16 = (pl.ds(0, KS), pl.ds(0, KB))
+    rows_out = (pl.ds(0, KS), pl.ds(KS, KP))
+
     local = pltpu.make_async_copy
 
-    in_copies = [local(w_in.at[c], w.at[0], in_sem.at[0]),
+    y_cols = pl.ds(pl.multiple_of(z * (2 * H), 2 * H), 2 * H)
+    in_copies = [local(w_in, raw.at[0], in_sem.at[0]),
                  local(eta_in, eta.at[0], in_sem.at[1]),
-                 local(y_in, res, in_sem.at[2])]
+                 local(y_in.at[:, :, y_cols], yraw, in_sem.at[2])]
     for cp in in_copies:
         cp.start()
 
@@ -66,7 +99,7 @@
         pl.semaphore_signal(bar, inc=1, device_id=dev, device_id_type=MESH)
     pl.semaphore_wait(bar, 3)
 
-    w_x = remote(w_in.at[1 - c], w.at[1], in_sem.at[3], in_sem.at[4], pal)
+    w_x = remote(w_in, raw.at[1], in_sem.at[3], in_sem.at[4], pal)
     e_x = remote(eta_in, eta.at[1], in_sem.at[5], in_sem.at[6], pal)
     w_x.start()
     e_x.start()
@@ -85,8 +118,24 @@
     def to_half(v):
         return jnp.concatenate([v, jnp.zeros((KB - KP, v.shape[1]), jnp.float32)], axis=0).astype(jnp.bfloat16)
 
+    mine = pl.ds(pl.multiple_of(c * KS, 8), KP)
+
+    def flatten(src):
+        wide = src.shape[2]
+        flat[0:K, 0:wide] = src[:, 0, :]
+        flat[K:2 * K, 0:wide] = src[:, 1, :]
+
     for b in range(2):
+        flatten(raw.at[b])
+        w[b] = flat[mine, 0:DP]
         dwb[b] = to_half(w[b])
+    flatten(yraw)
+    for h in range(2):
+        res[h] = flat[mine, h * H:(h + 1) * H]
+
+    @pl.when(c == 1)
+    def _():
+        pl.semaphore_wait(go_sem, 1)
 
     CB = 256
 
@@ -110,10 +159,10 @@
                 g[b, :, cols] += part[:KP]
 
     def rs_up(m, src):
-        return remote(src, rup.at[m], rsu_s.at[m], rsu_r.at[m], up)
+        return Split(lambda q: remote(src.at[rows32[q]], rup.at[m, rows32[q]], rsu_s.at[m], rsu_r.at[m], up))
 
     def rs_dn(m, src):
-        return remote(src, rdn.at[m], rsd_s.at[m], rsd_r.at[m], dn)
+        return Split(lambda q: remote(src.at[rows32[q]], rdn.at[m, rows32[q]], rsd_s.at[m], rsd_r.at[m], dn))
 
     def ring_step(m, t, with_recv, with_send):
         ku, kd = up_chunk(m), dn_chunk(m)
@@ -145,6 +194,10 @@
 
         def rest(m, _):
             ring_step(m, t, True, True)
+
+            @pl.when((t == 0) & (m == STAGGER) & (c == 0))
+            def _():
+                pl.semaphore_signal(go_sem, inc=1, device_id=pal, device_id_type=MESH)
             return 0
         lax.fori_loop(0, 2, first, 0)
         lax.fori_loop(2, hops, rest, 0)
@@ -165,12 +218,12 @@
             return 0
         lax.fori_loop(0, hops, drain, 0)
 
-    def gather_ring(buf, us, ur, ds, dr, seen):
+    def gather_ring(buf, rows, us, ur, ds, dr, seen):
         def send_up(m, k):
-            return remote(buf.at[k], buf.at[k], us.at[m], ur.at[m], up)
+            return Split(lambda q: remote(buf.at[k, rows[q]], buf.at[k, rows[q]], us.at[m], ur.at[m], up))
 
         def send_dn(m, k):
-            return remote(buf.at[k], buf.at[k], ds.at[m], dr.at[m], dn)
+            return Split(lambda q: remote(buf.at[k, rows[q]], buf.at[k, rows[q]], ds.at[m], dr.at[m], dn))
         k0, k1 = chunk(0, 0), chunk(0, 1)
         send_up(0, k0).start()
         send_dn(0, k1).start()
@@ -203,7 +256,8 @@
             return 0
         lax.fori_loop(0, hops, drain, 0)
 
-    lam = jnp.where(c == 0, jnp.float32(lams[0]), jnp.float32(lams[1]))
+    first = lax.broadcasted_iota(jnp.int32, (KP, 1), 0) + c * KS < K
+    lam = jnp.where(first, jnp.float32(LAMS[0]), jnp.float32(LAMS[1]))
 
     def one_round(t, _):
         reduce_round(t)
@@ -212,72 +266,109 @@
         def _():
             for h in range(2):
                 gat[chunk(0, h)] = to_half(res[h])
-            gather_ring(gat, agu_s, agu_r, agd_s, agd_r, gradient)
+            gather_ring(gat, rows16, agu_s, agu_r, agd_s, agd_r, gradient)
             for b in range(2):
                 for j in range(DP // CB):
                     cols = pl.ds(j * CB, CB)
                     old = w[b, :, cols]
-                    step = eta[b, 0:1, cols] * (g[b, :, cols] * (1.0 / N) - lam * old)
+                    step = eta[b, :, cols] * (g[b, :, cols] * (1.0 / N) - lam * old)
                     w[b, :, cols] = old + step
                     dwb[b, :, cols] = to_half(step)
         return 0
 
     lax.fori_loop(0, SWEEPS + 1, one_round, 0)
 
-    w_own = local(w.at[0], w_res.at[c], wo_sem.at[0])
-    w_pal = remote(w.at[1], w_res.at[c], wo_sem.at[1], wo_sem.at[2], pal)
+    def w_own_copy(q):
+        return local(w.at[0, rows32[q]], w_res.at[rows_out[q]], wo_sem.at[0])
+
+    def w_pal_copy(q):
+        return remote(w.at[1, rows32[q]], w_res.at[rows_out[q]], wo_sem.at[1], wo_sem.at[2], pal)
+    w_own, w_pal = Split(w_own_copy), Split(w_pal_copy)
     w_own.start()
     w_pal.start()
     for h in range(2):
         rf[chunk(0, h)] = res[h]
 
     def out_local(k):
-        return local(rf.at[k], r_res.at[c, k], lo_s.at[k])
+        return Split(lambda q: local(rf.at[k, rows32[q]], r_res.at[k, rows_out[q]], lo_s.at[k]))
 
     def out_pal(k):
-        return remote(rf.at[k], r_res.at[c, k], po_s.at[k], po_r.at[k], pal)
+        return Split(lambda q: out_pal_copy(k, q))
+
+    def out_pal_copy(k, q):
+        return remote(rf.at[k, rows32[q]], r_res.at[k, rows_out[q]], po_s.at[k], po_r.at[k], pal)
 
     def emit(k):
         out_pal(k).start()
         out_local(k).start()
-    gather_ring(rf, fgu_s, fgu_r, fgd_s, fgd_r, emit)
+    gather_ring(rf, rows32, fgu_s, fgu_r, fgd_s, fgd_r, emit)
 
     def finish(k, _):
         out_local(k).wait()
-        out_pal(k).wait()
+        out_pal(k).wait_send()
+        Split(lambda q: out_pal_copy(k, 1 - q)).wait_recv()
         xp_copy(k).wait_send()
         return 0
     lax.fori_loop(0, 2 * Z, finish, 0)
     w_own.wait()
-    w_pal.wait()
-
-
-def _fused(x, wt, eta, ysh, Z, KP, KB, H, DP, N):
+    w_pal.do(lambda cp: cp.wait_send())
+    Split(lambda q: w_pal_copy(1 - q)).wait_recv()
+
+
+def _fused(x, wt, eta, yt, cfg):
+    Z, KS, KP, KB, H, DP, N = cfg
+    K = wt.shape[0]
     hops = Z - 1
     any_spec = pl.BlockSpec(memory_space=pl.ANY)
     f32, b16 = jnp.float32, jnp.bfloat16
     dma = pltpu.SemaphoreType.DMA
-    cfg = (Z, KP, KB, H, DP, N, (0.1, 1.0))
     scratch = [
         pltpu.VMEM((2 * Z, H, DP), b16), pltpu.VMEM((2 * Z, H, DP), b16),
         pltpu.VMEM((2 * Z, KP, H), f32),
         pltpu.VMEM((hops, KP, H), f32), pltpu.VMEM((hops, KP, H), f32),
         pltpu.VMEM((2 * Z, KB, H), b16),
         pltpu.VMEM((2, KP, DP), f32), pltpu.VMEM((2, KP, DP), f32), pltpu.VMEM((2, KB, DP), b16),
-        pltpu.VMEM((2, 8, DP), f32), pltpu.VMEM((2, KP, H), f32),
+        pltpu.VMEM((2, 1, DP), f32), pltpu.VMEM((2, KP, H), f32),
         pltpu.VMEM((2 * Z, KP, H), f32),
         dma((2 * Z,)), dma((2 * Z,)), dma((2 * Z,)), dma((7,)),
-    ] + [dma((hops,))] * 12 + [dma((2 * Z,)), dma((2 * Z,)), dma((2 * Z,)), dma((3,))]
+    ] + [dma((hops,))] * 12 + [dma((2 * Z,)), dma((2 * Z,)), dma((2 * Z,)), dma((3,))] + [
+        pltpu.VMEM((2, K, 2, DP), f32), pltpu.VMEM((K, 2, 2 * H), f32),
+        pltpu.VMEM((2 * K, max(DP, 2 * H)), f32), pltpu.SemaphoreType.REGULAR,
+    ]
     flops = (SWEEPS * 2 + 1) * 2 * N * DP * 2 * KP
     return pl.pallas_call(
         functools.partial(_kernel, cfg),
-        out_shape=(jax.ShapeDtypeStruct((2, KP, DP), f32), jax.ShapeDtypeStruct((2, 2 * Z, KP, H), f32)),
+        out_shape=(jax.ShapeDtypeStruct((2 * K, DP), f32), jax.ShapeDtypeStruct((2 * Z, 2 * K, H), f32)),
         in_specs=[any_spec] * 4,
         out_specs=(any_spec, any_spec),
         scratch_shapes=scratch,
         compiler_params=pltpu.CompilerParams(collective_id=0, has_side_effects=True, vmem_limit_bytes=64000000),
         cost_estimate=pl.CostEstimate(flops=flops, bytes_accessed=2 * N * DP * 2, transcendentals=0),
-    )(x, wt, eta, ysh)
+    )(x, wt, eta, yt)
+
+
+def _arrange_kernel(K, H, w_flat, r_flat, w_new, r_new):
+    @pl.when(pl.program_id(0) == 0)
+    def _():
+        for q in range(2):
+            w_new[:, q, :] = w_flat[q * K:(q + 1) * K]
+    for i in range(r_flat.shape[0]):
+        for q in range(2):
+            r_new[:, q, i * H:(i + 1) * H] = r_flat[i, q * K:(q + 1) * K]
+
+
+def _arrange(w_flat, r_flat):
+    K2, DP = w_flat.shape
+    chunks, _, H = r_flat.shape
+    K, per = K2 // 2, 2
+    f32 = jnp.float32
+    return pl.pallas_call(
+        functools.partial(_arrange_kernel, K, H),
+        grid=(chunks // per,),
+        in_specs=[pl.BlockSpec((K2, DP), lambda i: (0, 0)), pl.BlockSpec((per, K2, H), lambda i: (i, 0, 0))],
+        out_specs=(pl.BlockSpec((K, 2, DP), lambda i: (0, 0, 0)), pl.BlockSpec((K, 2, per * H), lambda i: (0, 0, i))),
+        out_shape=(jax.ShapeDtypeStruct((K, 2, DP), f32), jax.ShapeDtypeStruct((K, 2, chunks * H), f32)),
+    )(w_flat, r_flat)
 
 
 def solution(mesh):
@@ -286,19 +377,16 @@
     def per_device(x_blk, w_blk, y_blk, eta_blk):
         N, DP = x_blk.shape
         K = y_blk.shape[2]
-        KP = -(-K // 8) * 8
-        KB = -(-K // 16) * 16
+        KS = K // 16 * 16
+        KP = 2 * K - KS
+        KB = -(-KP // 16) * 16
         H = N // (2 * Z)
-        me = lax.axis_index("feat")
-        z, c = me // 2, me % 2
-        wt = jnp.pad(jnp.transpose(w_blk, (1, 2, 0)), ((0, 0), (0, KP - K), (0, 0)))
-        ysh = lax.dynamic_slice(y_blk, (z * 2 * H, c, 0), (2 * H, 1, K)).reshape(2, H, K)
-        ysh = jnp.pad(jnp.transpose(ysh, (0, 2, 1)), ((0, 0), (0, KP - K), (0, 0)))
-        eta = jnp.broadcast_to(eta_blk[None, :], (8, DP))
-        w_t, r_t = _fused(x_blk.reshape(2 * Z, H, DP), wt, eta, ysh, Z, KP, KB, H, DP, N)
-        w_new = jnp.transpose(w_t[:, :K, :], (2, 0, 1))
-        r_new = jnp.transpose(r_t[:, :, :K, :], (1, 3, 0, 2)).reshape(N, 2, K)
-        return w_new, r_new
+        cfg = (Z, KS, KP, KB, H, DP, N)
+        wt = jnp.transpose(w_blk, (2, 1, 0))
+        yt = jnp.transpose(y_blk, (2, 1, 0))
+        w_flat, r_flat = _fused(x_blk.reshape(2 * Z, H, DP), wt, eta_blk.reshape(1, DP), yt, cfg)
+        w_new, r_new = _arrange(w_flat, r_flat)
+        return jnp.transpose(w_new, (2, 1, 0)), jnp.transpose(r_new, (2, 1, 0))
 
     x_spec = P("prob", "feat")
     w_spec = P(("prob", "feat"), None, None)

time: 330 us -> 293 us (0.89)
  local copies, waits for them, and re-layouts: 29.6 us -> 0 us
  Pallas kernels: 299 us -> 292 us
    unnamed x4 -> x0, local copies, waits for them, and re-layouts: 18.8 us -> none
    pallas_call x1, Pallas kernels: 299 us -> 283 us  [_fused(): pl.pallas_call(functools.partial(_kernel, cfg), out_shape=(jax.ShapeDtype...]
    pallas_call x0 -> x1, Pallas kernels: none -> 8.9 us  [_arrange(): pl.pallas_call(functools.partial(_arrange_kernel, K, H), grid=(chunks //...]
    transpose x2 -> x0, local copies, waits for them, and re-layouts: 4.95 us -> none  [the longest x1 3.72 us: per_device(): r_new = jnp.transpose(r_t[:, :, :K, :], (1, 3, 0, 2)).reshape(N, 2, K)]
where the time goes in v2:
time: 293 us
  Pallas kernels  292 us (100%)
    pallas_call x1, Pallas kernels, _fused(): pl.pallas_call(functools.partial(_kernel, cfg), out_shape=(jax.ShapeDtype...  283 us
    pallas_call x1, Pallas kernels, _arrange(): pl.pallas_call(functools.partial(_arrange_kernel, K, H), grid=(chunks //...  8.9 us

profile of v2, /device:TPU:21, one launch (start us, length us, event | category | flops | bytes accessed | tf_op | source)
XLA Modules:
  0.0 292.7 jit_solution(7387145368335907513)
XLA Ops:
  0.6 283.2 %shard_map.59 = (f32[200,1024]{1,0:T(8,128)}, f32[16,200,512]{2,1,0:T(8,128)}) custom-call(bf16[16,512,1024]{2,1,0:T(8,128)(2,1)} %bitcast.6, f32[100,2,1024]{2,1,0:T(2,128)} %bitcast.9, f32[1,1024]{1,0:T(1,128)} %bitcast.11, f32[100,2,8192]{2,1,0:T(2,128)} %bitcast.7), custom_call_target="tpu_custom_call" | custom-call | flops 31406948352 | bytes 33554432 | tf_op jit(solution)/shard_map/pallas_call | solution.py:339
  283.8 8.9 %shard_map.60 = (f32[100,2,1024]{2,1,0:T(2,128)}, f32[100,2,8192]{2,1,0:T(2,128)}) custom-call(f32[200,1024]{1,0:T(8,128)} %get-tuple-element.6.w_flat, f32[16,200,512]{2,1,0:T(8,128)} %get-tuple-element.7.r_flat), custom_call_target="tpu_custom_call" | custom-call | tf_op jit(solution)/shard_map/pallas_call | solution.py:365

commit v3 on v2

--- a/solution.py
+++ b/solution.py
@@ -9,7 +9,7 @@
 
 SWEEPS = 4
 LAMS = (0.1, 1.0)
-STAGGER = 2
+PIECES = 2
 MESH = pl.DeviceIdType.MESH
 
 
@@ -19,7 +19,7 @@
             rsu_s, rsu_r, rsd_s, rsd_r,
             agu_s, agu_r, agd_s, agd_r,
             fgu_s, fgu_r, fgd_s, fgd_r,
-            po_s, po_r, lo_s, wo_sem, raw, yraw, flat, go_sem):
+            po_s, po_r, lo_s, wo_sem, raw, yraw, flat):
     Z, KS, KP, KB, H, DP, N = cfg
     K = w_in.shape[0]
     hops = Z - 1
@@ -71,6 +71,8 @@
 
     rows32 = (pl.ds(0, KS), pl.ds(0, KP))
     rows16 = (pl.ds(0, KS), pl.ds(0, KB))
+    piece = H // PIECES
+    lanes = [pl.ds(i * piece, piece) for i in range(PIECES)]
     rows_out = (pl.ds(0, KS), pl.ds(KS, KP))
 
     local = pltpu.make_async_copy
@@ -132,10 +134,6 @@
     flatten(yraw)
     for h in range(2):
         res[h] = flat[mine, h * H:(h + 1) * H]
-
-    @pl.when(c == 1)
-    def _():
-        pl.semaphore_wait(go_sem, 1)
 
     CB = 256
 
@@ -158,11 +156,15 @@
                 part = jnp.dot(rows, xx[k, :, cols], preferred_element_type=jnp.float32)
                 g[b, :, cols] += part[:KP]
 
-    def rs_up(m, src):
-        return Split(lambda q: remote(src.at[rows32[q]], rup.at[m, rows32[q]], rsu_s.at[m], rsu_r.at[m], up))
-
-    def rs_dn(m, src):
-        return Split(lambda q: remote(src.at[rows32[q]], rdn.at[m, rows32[q]], rsd_s.at[m], rsd_r.at[m], dn))
+    def rs_up(m, src, i):
+        s = m * PIECES + i
+        return Split(lambda q: remote(src.at[rows32[q], lanes[i]], rup.at[m, rows32[q], lanes[i]],
+                                      rsu_s.at[s], rsu_r.at[s], up))
+
+    def rs_dn(m, src, i):
+        s = m * PIECES + i
+        return Split(lambda q: remote(src.at[rows32[q], lanes[i]], rdn.at[m, rows32[q], lanes[i]],
+                                      rsd_s.at[s], rsd_r.at[s], dn))
 
     def ring_step(m, t, with_recv, with_send):
         ku, kd = up_chunk(m), dn_chunk(m)
@@ -174,18 +176,21 @@
                 xp_copy(k).wait_recv()
         product(ku)
         if with_send and not with_recv:
-            rs_up(m, pf.at[ku]).start()
+            for i in range(PIECES):
+                rs_up(m, pf.at[ku], i).start()
         product(kd)
         if with_send and not with_recv:
-            rs_dn(m, pf.at[kd]).start()
+            for i in range(PIECES):
+                rs_dn(m, pf.at[kd], i).start()
         if with_recv:
             s = m - 2
-            rs_up(s, rup.at[s]).wait_recv()
-            rup[s] += pf[ku]
-            rs_up(m, rup.at[s]).start()
-            rs_dn(s, rdn.at[s]).wait_recv()
-            rdn[s] += pf[kd]
-            rs_dn(m, rdn.at[s]).start()
+            for i in range(PIECES):
+                rs_up(s, rup.at[s], i).wait_recv()
+                rup[s, :, lanes[i]] += pf[ku, :, lanes[i]]
+                rs_up(m, rup.at[s], i).start()
+                rs_dn(s, rdn.at[s], i).wait_recv()
+                rdn[s, :, lanes[i]] += pf[kd, :, lanes[i]]
+                rs_dn(m, rdn.at[s], i).start()
 
     def reduce_round(t):
         def first(m, _):
@@ -194,65 +199,71 @@
 
         def rest(m, _):
             ring_step(m, t, True, True)
-
-            @pl.when((t == 0) & (m == STAGGER) & (c == 0))
-            def _():
-                pl.semaphore_signal(go_sem, inc=1, device_id=pal, device_id_type=MESH)
             return 0
         lax.fori_loop(0, 2, first, 0)
         lax.fori_loop(2, hops, rest, 0)
         ring_step(hops, t, False, False)
         g[...] = jnp.zeros_like(g)
         a, b = hops - 2, hops - 1
-        rs_up(a, rup.at[a]).wait_recv()
-        rs_dn(a, rdn.at[a]).wait_recv()
-        rs_up(b, rup.at[b]).wait_recv()
+        for i in range(PIECES):
+            rs_up(a, rup.at[a], i).wait_recv()
+            rs_dn(a, rdn.at[a], i).wait_recv()
+        for i in range(PIECES):
+            rs_up(b, rup.at[b], i).wait_recv()
         k0, k1 = chunk(0, 0), chunk(0, 1)
         res[0] = res[0] - (rup[b] + rdn[a] + pf[k0])
-        rs_dn(b, rdn.at[b]).wait_recv()
+        for i in range(PIECES):
+            rs_dn(b, rdn.at[b], i).wait_recv()
         res[1] = res[1] - (rup[a] + rdn[b] + pf[k1])
 
         def drain(m, _):
-            rs_up(m, rup.at[m]).wait_send()
-            rs_dn(m, rdn.at[m]).wait_send()
+            for i in range(PIECES):
+                rs_up(m, rup.at[m], i).wait_send()
+                rs_dn(m, rdn.at[m], i).wait_send()
             return 0
         lax.fori_loop(0, hops, drain, 0)
 
     def gather_ring(buf, rows, us, ur, ds, dr, seen):
-        def send_up(m, k):
-            return Split(lambda q: remote(buf.at[k, rows[q]], buf.at[k, rows[q]], us.at[m], ur.at[m], up))
-
-        def send_dn(m, k):
-            return Split(lambda q: remote(buf.at[k, rows[q]], buf.at[k, rows[q]], ds.at[m], dr.at[m], dn))
+        def send_up(m, k, i):
+            s = m * PIECES + i
+            return Split(lambda q: remote(buf.at[k, rows[q], lanes[i]], buf.at[k, rows[q], lanes[i]],
+                                          us.at[s], ur.at[s], up))
+
+        def send_dn(m, k, i):
+            s = m * PIECES + i
+            return Split(lambda q: remote(buf.at[k, rows[q], lanes[i]], buf.at[k, rows[q], lanes[i]],
+                                          ds.at[s], dr.at[s], dn))
         k0, k1 = chunk(0, 0), chunk(0, 1)
-        send_up(0, k0).start()
-        send_dn(0, k1).start()
-        send_up(1, k1).start()
-        send_dn(1, k0).start()
+        for m, ku, kd in ((0, k0, k1), (1, k1, k0)):
+            for i in range(PIECES):
+                send_up(m, ku, i).start()
+                send_dn(m, kd, i).start()
         seen(k0)
         seen(k1)
 
         def step(m, _):
             far = lax.div(m, 2) + 1
             ku, kd = chunk(-far, lax.rem(m, 2)), chunk(far, 1 - lax.rem(m, 2))
-            send_up(m, ku).wait_recv()
-
-            @pl.when(m < hops - 2)
-            def _():
-                send_up(m + 2, ku).start()
-            send_dn(m, kd).wait_recv()
-
-            @pl.when(m < hops - 2)
-            def _():
-                send_dn(m + 2, kd).start()
+            for i in range(PIECES):
+                send_up(m, ku, i).wait_recv()
+
+                @pl.when(m < hops - 2)
+                def _():
+                    send_up(m + 2, ku, i).start()
+                send_dn(m, kd, i).wait_recv()
+
+                @pl.when(m < hops - 2)
+                def _():
+                    send_dn(m + 2, kd, i).start()
             seen(ku)
             seen(kd)
             return 0
         lax.fori_loop(0, hops, step, 0)
 
         def drain(m, _):
-            send_up(m, k0).wait_send()
-            send_dn(m, k0).wait_send()
+            for i in range(PIECES):
+                send_up(m, k0, i).wait_send()
+                send_dn(m, k0, i).wait_send()
             return 0
         lax.fori_loop(0, hops, drain, 0)
 
@@ -331,9 +342,9 @@
         pltpu.VMEM((2, 1, DP), f32), pltpu.VMEM((2, KP, H), f32),
         pltpu.VMEM((2 * Z, KP, H), f32),
         dma((2 * Z,)), dma((2 * Z,)), dma((2 * Z,)), dma((7,)),
-    ] + [dma((hops,))] * 12 + [dma((2 * Z,)), dma((2 * Z,)), dma((2 * Z,)), dma((3,))] + [
+    ] + [dma((hops * PIECES,))] * 12 + [dma((2 * Z,)), dma((2 * Z,)), dma((2 * Z,)), dma((3,))] + [
         pltpu.VMEM((2, K, 2, DP), f32), pltpu.VMEM((K, 2, 2 * H), f32),
-        pltpu.VMEM((2 * K, max(DP, 2 * H)), f32), pltpu.SemaphoreType.REGULAR,
+        pltpu.VMEM((2 * K, max(DP, 2 * H)), f32),
     ]
     flops = (SWEEPS * 2 + 1) * 2 * N * DP * 2 * KP
     return pl.pallas_call(
@@ -347,27 +358,59 @@
     )(x, wt, eta, yt)
 
 
-def _arrange_kernel(K, H, w_flat, r_flat, w_new, r_new):
-    @pl.when(pl.program_id(0) == 0)
-    def _():
+def _arrange_kernel(K, H, w_flat, r_flat, w_new, r_new, w_a, r_a, w_b, r_b, sem_a, sem_b):
+    chunks = r_flat.shape[0]
+    local = pltpu.make_async_copy
+
+    def load(i):
+        return local(r_flat.at[i], r_a.at[i], sem_a.at[i])
+
+    def store(i):
+        cols = pl.ds(pl.multiple_of(i * H, H), H)
+        return local(r_b.at[i], r_new.at[:, :, cols], sem_b.at[i])
+    w_load = local(w_flat, w_a, sem_a.at[chunks])
+    w_store = local(w_b, w_new, sem_b.at[chunks])
+    w_load.start()
+
+    def begin(i, _):
+        load(i).start()
+        return 0
+    lax.fori_loop(0, chunks, begin, 0)
+    w_load.wait()
+    for q in range(2):
+        w_b[:, q, :] = w_a[q * K:(q + 1) * K]
+    w_store.start()
+
+    def move(i, _):
+        load(i).wait()
         for q in range(2):
-            w_new[:, q, :] = w_flat[q * K:(q + 1) * K]
-    for i in range(r_flat.shape[0]):
-        for q in range(2):
-            r_new[:, q, i * H:(i + 1) * H] = r_flat[i, q * K:(q + 1) * K]
+            r_b[i, :, q, :] = r_a[i, q * K:(q + 1) * K]
+        store(i).start()
+        return 0
+    lax.fori_loop(0, chunks, move, 0)
+
+    def end(i, _):
+        store(i).wait()
+        return 0
+    lax.fori_loop(0, chunks, end, 0)
+    w_store.wait()
 
 
 def _arrange(w_flat, r_flat):
     K2, DP = w_flat.shape
     chunks, _, H = r_flat.shape
-    K, per = K2 // 2, 2
+    K = K2 // 2
     f32 = jnp.float32
+    any_spec = pl.BlockSpec(memory_space=pl.ANY)
     return pl.pallas_call(
         functools.partial(_arrange_kernel, K, H),
-        grid=(chunks // per,),
-        in_specs=[pl.BlockSpec((K2, DP), lambda i: (0, 0)), pl.BlockSpec((per, K2, H), lambda i: (i, 0, 0))],
-        out_specs=(pl.BlockSpec((K, 2, DP), lambda i: (0, 0, 0)), pl.BlockSpec((K, 2, per * H), lambda i: (0, 0, i))),
+        in_specs=[any_spec, any_spec],
+        out_specs=(any_spec, any_spec),
         out_shape=(jax.ShapeDtypeStruct((K, 2, DP), f32), jax.ShapeDtypeStruct((K, 2, chunks * H), f32)),
+        scratch_shapes=[pltpu.VMEM((K2, DP), f32), pltpu.VMEM((chunks, K2, H), f32),
+                        pltpu.VMEM((K, 2, DP), f32), pltpu.VMEM((chunks, K, 2, H), f32),
+                        pltpu.SemaphoreType.DMA((chunks + 1,)), pltpu.SemaphoreType.DMA((chunks + 1,))],
+        compiler_params=pltpu.CompilerParams(vmem_limit_bytes=64000000),
     )(w_flat, r_flat)
 
 

time: 293 us -> 295 us (level)
    pallas_call x1, Pallas kernels: 283 us -> 288 us  [_fused(): pl.pallas_call(functools.partial(_kernel, cfg), out_shape=(jax.ShapeDtype...]
where the time goes in v3:
time: 295 us
  Pallas kernels  294 us (100%)
    pallas_call x1, Pallas kernels, _fused(): pl.pallas_call(functools.partial(_kernel, cfg), out_shape=(jax.ShapeDtype...  288 us
    pallas_call x1, Pallas kernels, _arrange(): pl.pallas_call(functools.partial(_arrange_kernel, K, H), in_specs=[any_sp...  6.36 us

profile of v3, /device:TPU:21, one launch (start us, length us, event | category | flops | bytes accessed | tf_op | source)
XLA Modules:
  0.0 294.7 jit_solution(13446857297735621557)
XLA Ops:
  0.6 287.7 %shard_map.59 = (f32[200,1024]{1,0:T(8,128)}, f32[16,200,512]{2,1,0:T(8,128)}) custom-call(bf16[16,512,1024]{2,1,0:T(8,128)(2,1)} %bitcast.6, f32[100,2,1024]{2,1,0:T(2,128)} %bitcast.9, f32[1,1024]{1,0:T(1,128)} %bitcast.11, f32[100,2,8192]{2,1,0:T(2,128)} %bitcast.7), custom_call_target="tpu_custom_call" | custom-call | flops 31406948352 | bytes 33554432 | tf_op jit(solution)/shard_map/pallas_call | solution.py:350
  288.4 6.4 %shard_map.60 = (f32[100,2,1024]{2,1,0:T(2,128)}, f32[100,2,8192]{2,1,0:T(2,128)}) custom-call(f32[200,1024]{1,0:T(8,128)} %get-tuple-element.6.w_flat, f32[16,200,512]{2,1,0:T(8,128)} %get-tuple-element.7.r_flat), custom_call_target="tpu_custom_call" | custom-call | tf_op jit(solution)/shard_map/pallas_call | solution.py:405
